TPU v7x, 32 devices: a whole 2x2x4 slice. The times are simulated.
32 devices in a mesh: row: 4 (over y, x), col: 2 (over core), layer: 4 (over z).
Axes of the slice: x: 2, y: 2, z: 4, core: 2. Of those that a mesh axis runs over, the one named last changes fastest.
Arguments:
- matrix: float32 [4096, 4096], P('row', 'col'), may hold values from -6 to 6
- pattern: int32 [128, 128], P('row', 'col'), may hold values 0 or 1
- keep: int32 [128, 128], P('row', 'col'), may hold values 0 or 1
Outputs:
- update: float32 [4096, 4096], P(('row', 'layer'), 'col')
All inputs are finite; a program needn't handle non-finite values. No bound on the sum of `pattern` or of `keep` on one device may be relied on, other than what follows from the above.
Results may differ from a plain program's by a relative error of at most 0.00005.
Values sent between devices are 32-bit elements; how exact they have to be, the bound alone decides.
A program may use at most 128 MiB of HBM per device.

v0:
```python
import jax
import jax.numpy as jnp
from jax import lax
from jax.sharding import PartitionSpec as P

BS = 32
NB = 128


def layer_rows(values, layers, level):
    count, width = values.shape
    shaped = values.reshape(count // (layers * BS), layers, BS, width)
    picked = lax.dynamic_index_in_dim(shaped, level, 1, keepdims=False)
    return picked.reshape(count // layers, width)


def local(matrix, pattern, keep):
    rows, cols = matrix.shape
    block_rows, block_cols = pattern.shape
    layers = lax.axis_size("layer")
    level = lax.axis_index("layer")
    sparse = (
        matrix.reshape(block_rows, BS, block_cols, BS)
        * pattern.astype(jnp.float32)[:, None, :, None]
    ).reshape(rows, cols)
    left_local = lax.dynamic_index_in_dim(
        sparse.reshape(rows, block_cols // layers, layers, BS), level, 2, keepdims=False
    )
    left_local = left_local.reshape(rows, block_cols // layers * BS)
    left_full = lax.all_gather(left_local, "col", axis=1, tiled=True)
    right_full = lax.all_gather(layer_rows(sparse, layers, level), "row", axis=0, tiled=True)
    partial_value = jnp.dot(
        left_full, right_full, preferred_element_type=jnp.float32, precision=lax.Precision.HIGH
    )
    keep_flags = keep.astype(jnp.float32)
    keep_mine = lax.dynamic_index_in_dim(
        keep_flags.reshape(block_rows // layers, layers, block_cols), level, 1, keepdims=False
    )
    by_layer = partial_value.reshape(block_rows // layers, layers, BS, cols).transpose(1, 0, 2, 3)
    mine = lax.psum_scatter(
        by_layer.reshape(rows, cols), "layer", scatter_dimension=0, tiled=True
    )
    filtered = (
        mine.reshape(block_rows // layers, BS, block_cols, BS) * keep_mine[:, None, :, None]
    ).reshape(rows // layers, cols)
    filtered_full = lax.all_gather(filtered, "row", axis=0, tiled=True)
    share = rows // layers
    summed = lax.psum_scatter(
        jnp.dot(
            left_full,
            filtered_full,
            preferred_element_type=jnp.float32,
            precision=lax.Precision.HIGH,
        ),
        "layer",
        scatter_dimension=0,
        tiled=True,
    )
    own_rows = lax.dynamic_slice_in_dim(sparse, level * share, share, 0)
    factor = 0.72 / (NB * BS)
    return 1.5 * own_rows - 0.5 * factor * summed


def solution(mesh):
    placed = (P("row", "col"), P("row", "col"), P("row", "col"))
    return jax.shard_map(
        local, mesh=mesh, in_specs=placed, out_specs=P(("row", "layer"), "col"), check_vma=False
    )
```

profile of v0, /device:TPU:12, one launch (start us, length us, event | category | flops | bytes accessed | tf_op | source)
XLA Modules:
  0.0 557.1 jit_solution(13502446609699732119)
XLA Ops:
  6.5 0.0 all-gather.4.cloned.1.call-start
  6.5 0.7 convert_element_type.6
  7.3 9.3 %copy.4 = f32[1024,2048]{0,1:T(8,128)} copy(f32[1024,2048]{1,0:T(8,128)} %param.3) | data formatting | bytes 16777216 | tf_op args[0]
  16.5 0.1 copy.5
  16.6 0.3 mul.63
  16.9 0.5 mul.64
  17.4 0.1 constant_dynamic-slice_fusion.2
  17.5 3.3 dynamic-slice_multiply_fusion.1
  20.8 0.0 all-gather.4.cloned.1.call-update
  20.8 0.0 all-gather.6.cloned.1.call-start
  20.9 0.3 mul.67
  21.2 0.5 mul.68
  21.7 0.1 constant_dynamic-slice_fusion.1
  21.8 3.3 dynamic-slice_multiply_fusion
  25.0 0.0 all-gather.6.cloned.1.call-update
  25.1 0.0 reduce-scatter.3.cloned.1.call-start
  25.1 10.9 %all-gather.4.cloned.1.call-done = f32[1024,1024]{0,1:T(8,128)} async-done(((f32[1024,512]{0,1:T(8,128)}), f32[1024,1024]{0,1:T(8,128)}) %all-gather.4.cloned.1.call-update) | async-done | bytes 4194320 | tf_op jit(solution)/shard_map/all_gather | solution.py:30
  36.0 90.3 %all-gather.6.cloned.1.call-done = f32[1024,2048]{1,0:T(8,128)} async-done(((f32[256,2048]{1,0:T(8,128)}), f32[1024,2048]{1,0:T(8,128)}) %all-gather.6.cloned.1.call-update) | async-done | bytes 8388624 | tf_op jit(solution)/shard_map/all_gather | solution.py:31
  126.3 16.8 %fusion.2 = f32[1024,2048]{1,0:T(8,128)S(1)} fusion(f32[1024,1024]{0,1:T(8,128)} %all-gather.4.cloned.1.call-done, f32[1024,2048]{1,0:T(8,128)} %all-gather.6.cloned.1.call-done), kind=kOutput, calls=%fused_computation.8 | convolution fusion | flops 12884901888 | bytes 20971520 | tf_op jit(solution)/shard_map/dot_general | solution.py:32
  143.1 3.8 copy.6
  146.9 0.0 copy-start
  146.9 0.0 reduce-scatter.3.cloned.1.call-update
  146.9 0.0 all-gather.8.cloned.1.call-start
  146.9 0.6 copy-done
  147.6 4.4 mul.72
  152.0 6.7 %mul.73 = f32[256,2048]{1,0:T(8,128)S(1)} reshape(f32[8,32,64,32]{3,2,1,0:T(8,128)} %mul.72) | data formatting | bytes 4194304 | tf_op jit(solution)/shard_map/mul | solution.py:44
  158.7 132.6 %reduce-scatter.3.cloned.1.call-done = f32[256,2048]{1,0:T(8,128)} async-done(((f32[1024,2048]{1,0:T(8,128)}), f32[256,2048]{1,0:T(8,128)}) %reduce-scatter.3.cloned.1.call-update) | async-done | bytes 2097168 | tf_op jit(solution)/shard_map/reduce_scatter | solution.py:40
  291.2 3.2 mul.74
  294.4 0.0 all-gather.8.cloned.1.call-update
  294.4 0.2 reduce-scatter.5.cloned.1.call-start
  294.7 88.4 %all-gather.8.cloned.1.call-done = f32[1024,2048]{1,0:T(8,128)} async-done(((f32[256,2048]{1,0:T(8,128)}), f32[1024,2048]{1,0:T(8,128)}) %all-gather.8.cloned.1.call-update) | async-done | bytes 8388624 | tf_op jit(solution)/shard_map/all_gather | solution.py:46
  383.1 18.1 %fusion.3 = f32[1024,2048]{1,0:T(8,128)} fusion(f32[1024,1024]{0,1:T(8,128)} %all-gather.4.cloned.1.call-done, f32[1024,2048]{1,0:T(8,128)} %all-gather.8.cloned.1.call-done), kind=kOutput, calls=%fused_computation.9 | convolution fusion | flops 12884901888 | bytes 20971520 | tf_op jit(solution)/shard_map/dot_general | solution.py:49
  401.2 0.0 reduce-scatter.5.cloned.1.call-update
  401.2 11.7 %mul.57 = f32[32,32,64,32]{3,2,1,0:T(8,128)} broadcast(f32[32,64]{1,0:T(8,128)S(1)} %convert_element_type.6), dimensions={0,2} | broadcast | bytes 8396800 | tf_op jit(solution)/shard_map/mul | solution.py:23
  412.9 25.5 %mul.58 = f32[1024,2048]{1,0:T(8,128)} reshape(f32[32,32,64,32]{3,2,1,0:T(8,128)} %mul.57) | data formatting | bytes 16777216 | tf_op jit(solution)/shard_map/mul | solution.py:23
  438.3 107.2 %reduce-scatter.5.cloned.1.call-done = f32[256,2048]{1,0:T(8,128)} async-done(((f32[1024,2048]{1,0:T(8,128)}), f32[256,2048]{1,0:T(8,128)}) %reduce-scatter.5.cloned.1.call-update) | async-done | bytes 2097168 | tf_op jit(solution)/shard_map/reduce_scatter | solution.py:48
  545.6 5.0 fusion.1
  (2 shorter events, 0.0 us)
Async XLA Ops:
  6.5 29.5 %all-gather.4.cloned.1.call-start = ((), (), s32[]{:S(2)}) async-start(), calls=%async_computation.2 | async-start | bytes 6291456 | tf_op jit(solution)/shard_map/all_gather | solution.py:30
  20.8 105.5 %all-gather.6.cloned.1.call-start = ((), (), s32[]{:S(2)}) async-start(), calls=%async_computation.3 | async-start | bytes 10485760 | tf_op jit(solution)/shard_map/all_gather | solution.py:31
  25.1 266.2 %reduce-scatter.3.cloned.1.call-start = ((), (), s32[]{:S(2)}) async-start(), calls=%async_computation.4 | async-start | bytes 10485760 | tf_op jit(solution)/shard_map/reduce_scatter | solution.py:40
  146.9 0.7 copy-start
  146.9 236.2 %all-gather.8.cloned.1.call-start = ((), (), s32[]{:S(2)}) async-start(), calls=%async_computation.5 | async-start | bytes 10485760 | tf_op jit(solution)/shard_map/all_gather | solution.py:46
  294.4 251.1 %reduce-scatter.5.cloned.1.call-start = ((), (), s32[]{:S(2)}) async-start(), calls=%async_computation.6 | async-start | bytes 10485760 | tf_op jit(solution)/shard_map/reduce_scatter | solution.py:48
Sparse Core Ops, SparseCore 0:
  20.9 15.0 all-gather.3
  37.9 88.3 all-gather.5
  147.0 144.1 reduce-scatter.2
  294.5 88.4 all-gather.7
  401.3 144.1 reduce-scatter.4
where the time goes:
time: 560 us; the launch traced here: 557 us
  waiting for transfers between devices  429 us (77%)
  local copies, waits for them, and re-layouts  63.8 us (11%)
  matrix products  34.9 us (6%)
  other arithmetic  15.4 us (3%)
  between operations  13.2 us (2%)
    reduce_scatter x1, waiting for transfers between devices, local(): lax.psum_scatter(by_layer.reshape(rows, cols), 'layer', scatter_dimension...  133 us
    reduce_scatter x1, waiting for transfers between devices, local(): lax.psum_scatter(jnp.dot(left_full, filtered_full, preferred_element_type...  107 us
    all_gather x1, waiting for transfers between devices, local(): lax.all_gather(layer_rows(sparse, layers, level), 'row', axis=0, tiled=True)  90.3 us
    all_gather x1, waiting for transfers between devices, local(): filtered_full = lax.all_gather(filtered, 'row', axis=0, tiled=True)  88.4 us
    mul x6, local copies, waits for them, and re-layouts, local(): matrix.reshape(block_rows, BS, block_cols, BS)  38.8 us
    dot_general x1, matrix products, local(): jnp.dot(left_full, filtered_full, preferred_element_type=jnp.float32, pre...  18.1 us
    dot_general x1, matrix products, local(): jnp.dot(left_full, right_full, preferred_element_type=jnp.float32, precis...  16.8 us
  transfers between devices with their start and end apart: 5, of which 5 were waited for; matrix products, arithmetic and copies ran while one was open for 9% of the time, Pallas kernels for 0%

commit v1 on v0

v1 whole, which is shorter than its diff:
```python
import functools

import jax
import jax.numpy as jnp
from jax import lax
from jax.experimental import pallas as pl
from jax.experimental.pallas import tpu as pltpu
from jax.sharding import PartitionSpec as P

MESH = pl.DeviceIdType.MESH
LANES = 128
DAMPING = 0.72


def masked(values, flags):
    rows, cols = values.shape
    block_rows, block_cols = flags.shape
    shaped = values.reshape(block_rows, rows // block_rows, block_cols, cols // block_cols)
    return (shaped * flags.astype(jnp.float32)[:, None, :, None]).reshape(rows, cols)


def plain(matrix, pattern, keep):
    rows, cols = matrix.shape
    layers = lax.axis_size("layer")
    level = lax.axis_index("layer")
    width = cols // layers
    flags = pattern.shape[1] // layers
    sparse = masked(matrix, pattern)
    left = lax.all_gather(sparse, "col", axis=1, tiled=True)
    mine = lax.dynamic_slice_in_dim(sparse, level * width, width, 1)
    right = lax.all_gather(mine, "row", axis=0, tiled=True)
    multiply = functools.partial(
        jnp.dot, preferred_element_type=jnp.float32, precision=lax.Precision.HIGH
    )
    filtered = masked(
        multiply(left, right), lax.dynamic_slice_in_dim(keep, level * flags, flags, 1)
    )
    product = multiply(left, lax.all_gather(filtered, "row", axis=0, tiled=True))
    factor = DAMPING / (rows * lax.axis_size("row"))
    update = 1.5 * mine - 0.5 * factor * product
    return lax.all_to_all(update, "layer", split_axis=0, concat_axis=1, tiled=True)


def split(values):
    high = values.astype(jnp.bfloat16)
    low = (values - high.astype(jnp.float32)).astype(jnp.bfloat16)
    return high, low


def kernel(
    layers, block, factor,
    matrix, pattern, keep, out,
    raw, panel, a_high, a_low, both, total, staged, flags_in, flags_a, flags_x, flags_keep,
    send_sem, recv_sem, panel_send, panel_recv, flag_send, flag_recv, out_send, out_recv, local_sem,
):
    rows, cols = matrix.shape
    chunks = cols // layers // LANES
    tasks = 2 * chunks
    half = rows // 2
    share = rows // layers
    block_rows = rows // block
    row = lax.axis_index("row")
    col = lax.axis_index("col")
    level = lax.axis_index("layer")
    y, x = row // 2, row % 2
    along_x = {"row": y * 2 + (1 - x)}
    along_y = {"row": (1 - y) * 2 + x}
    across = {"row": (1 - y) * 2 + (1 - x)}
    twin = {"col": 1 - col}
    others = [{"layer": (level + step) % layers} for step in range(1, layers)]

    barrier = pltpu.get_barrier_semaphore()
    peers = [along_x, along_y, across, twin] + others
    for peer in peers:
        pl.semaphore_signal(barrier, inc=1, device_id=peer, device_id_type=MESH)
    pl.semaphore_wait(barrier, len(peers))

    def remote(source, target, sent, landed, peer):
        return pltpu.make_async_remote_copy(
            src_ref=source, dst_ref=target, send_sem=sent, recv_sem=landed,
            device_id=peer, device_id_type=MESH,
        )

    def part(task, slot, top):
        return raw.at[task, slot, pl.ds(top * half, half)]

    def move(task, arrival, source):
        slot, top = ((1, 0), (1, 1), (2, 1), (2, 0), (3, 0), (3, 1))[arrival]
        peer = along_x if arrival in (0, 1, 5) else along_y
        return remote(
            source, part(task, slot, top), send_sem.at[task, arrival], recv_sem.at[task, arrival], peer
        )

    def own_x(task, top):
        start = pl.multiple_of((level * chunks + task) * LANES, LANES)
        return matrix.at[pl.ds(top * half, half), pl.ds(start, LANES)]

    def send_x(task):
        for arrival, top in ((0, 0), (2, 1), (1, 1), (3, 0)):
            move(task, arrival, own_x(task, top)).start()

    def send_f(task):
        for arrival, top in ((0, 0), (2, 1), (1, 1), (3, 0)):
            move(task, arrival, part(task, 0, top)).start()

    def hand_on(task):
        move(task, 0, part(task, 1, 0)).wait_recv()
        move(task, 4, part(task, 1, 0)).start()
        move(task, 2, part(task, 2, 1)).wait_recv()
        move(task, 5, part(task, 2, 1)).start()

    send_x(0)

    flag_moves = [
        remote(pattern, flags_in.at[n], flag_send.at[n], flag_recv.at[n], peer)
        for n, peer in enumerate((along_x, along_y, across, twin))
    ]
    for copy in flag_moves:
        copy.start()
    bands = 4
    tall = rows // bands

    def band(n):
        return pl.ds(n * tall, tall)

    panel_moves = [
        remote(matrix.at[band(n)], panel.at[1, band(n)], panel_send.at[n], panel_recv.at[n], twin)
        for n in range(bands)
    ]
    panel_local = [
        pltpu.make_async_copy(matrix.at[band(n)], panel.at[0, band(n)], local_sem.at[n])
        for n in range(bands)
    ]
    piece_local = [
        pltpu.make_async_copy(
            matrix.at[:, pl.ds(pl.multiple_of((level * chunks + n) * LANES, LANES), LANES)],
            raw.at[n, 0],
            local_sem.at[bands + n],
        )
        for n in range(chunks)
    ]
    for n in range(bands):
        panel_local[n].start()
        panel_moves[n].start()
    for copy in piece_local:
        copy.start()

    def expand(flags, first, width):
        index = lax.broadcasted_iota(jnp.int32, (flags.shape[1], width), 0)
        lane = lax.broadcasted_iota(jnp.int32, (flags.shape[1], width), 1)
        start = (index - first) * block
        table = jnp.where((lane >= start) & (lane < start + block), 1.0, 0.0)
        return jnp.dot(
            flags.astype(jnp.bfloat16), table.astype(jnp.bfloat16), preferred_element_type=jnp.float32
        )

    per_chunk = LANES // block

    def expand_chunks(flags, store):
        for n in range(chunks):
            store(n, expand(flags, (level * chunks + n) * per_chunk, LANES))

    def store_x(slot):
        def store(n, values):
            flags_x[n, slot] = values
        return store

    def store_keep(n, values):
        flags_keep[n] = values

    group = 8

    def prepare_panel(side, owner_col):
        for n in range(cols // half):
            owner = owner_col * (cols // rows) + n // 2
            slot = (owner // 2 + y) % 2 * 2 + (owner % 2 + x) % 2
            place = slot * 2 + n % 2

            def body(i, carry):
                flags = flags_a[side, pl.ds(pl.multiple_of(i * group, group), group), n * half : (n + 1) * half]
                for b in range(group):
                    at = pl.ds(pl.multiple_of((i * group + b) * block, block), block)
                    values = panel[side, at, n * half : (n + 1) * half] * flags[b : b + 1]
                    high, low = split(values)
                    a_high[place, at] = high
                    a_low[place, at] = low
                return carry

            lax.fori_loop(0, block_rows // group, body, 0)

    def take(task, slot, top):
        which = task - (task // chunks) * (task - chunks)

        def convert(i, carry):
            first = top * (half // block) + i * group
            flags = flags_x[which, slot, pl.ds(pl.multiple_of(first, group), group), :]
            for b in range(group):
                at = pl.ds(pl.multiple_of((first + b) * block, block), block)
                to = pl.ds(pl.multiple_of((i * group + b) * block, block), block)
                high, low = split(raw[task, slot, at, :] * flags[b : b + 1])
                both[to, 0:LANES] = high
                both[to, LANES : 2 * LANES] = low
            return carry

        lax.fori_loop(0, half // block // group, convert, 0)
        place = slot * 2 + top

        def multiply(i, carry):
            at = pl.ds(pl.multiple_of(i * half, half), half)
            total[at, :] += jnp.dot(
                a_high[place, at, :], both[...], preferred_element_type=jnp.float32
            ) + jnp.dot(a_low[place, at, :], both[...], preferred_element_type=jnp.float32)
            return carry

        lax.fori_loop(0, 2, multiply, 0)

    def finish(task):
        total[...] = jnp.zeros_like(total)

        def present(g, carry):
            take(task, g // 2 * (1 + g % 2), g % 2)
            return carry

        lax.fori_loop(0, 4, present, 0)
        for arrival, slot, top in ((3, 2, 0), (1, 1, 1), (4, 3, 0), (5, 3, 1)):
            move(task, arrival, part(task, slot, top)).wait_recv()
            if arrival == 1:
                late(task, 0)
            if arrival == 5:
                late(task, 2)

    def late(task, base):
        def body(g, carry):
            take(task, (1 - base // 2) * (2 - g) + base // 2 * 3, g)
            return carry

        lax.fori_loop(0, 2, body, 0)

    def block_loop(body):
        def step(i, carry):
            for b in range(group):
                body(i, b)
            return carry

        lax.fori_loop(0, block_rows // group, step, 0)

    def at_block(i, b):
        return pl.ds(pl.multiple_of((i * group + b) * block, block), block)

    def finish_square(task):
        finish(task)

        def body(i, b):
            flags = flags_keep[task, pl.ds(pl.multiple_of(i * group, group), group), :]
            at = at_block(i, b)
            summed = total[at, 0:LANES] + total[at, LANES : 2 * LANES]
            raw[task + chunks, 0, at, :] = summed * flags[b : b + 1]

        block_loop(body)

    def out_move(n, step):
        target = (level + step) % layers
        start = pl.multiple_of((level * chunks + n) * LANES, LANES)
        return remote(
            staged.at[n, pl.ds(pl.multiple_of(target * share, share), share)],
            out.at[:, pl.ds(start, LANES)],
            out_send.at[n, step - 1],
            out_recv.at[n, step - 1],
            {"layer": target},
        )

    def out_local(n):
        start = pl.multiple_of((level * chunks + n) * LANES, LANES)
        return pltpu.make_async_copy(
            staged.at[n, pl.ds(pl.multiple_of(level * share, share), share)],
            out.at[:, pl.ds(start, LANES)],
            local_sem.at[bands + chunks + n],
        )

    def finish_update(task):
        finish(task)
        n = task - chunks

        def body(i, b):
            flags = flags_x[n, 0, pl.ds(pl.multiple_of(i * group, group), group), :]
            at = at_block(i, b)
            summed = total[at, 0:LANES] + total[at, LANES : 2 * LANES]
            staged[n, at, :] = 1.5 * (raw[n, 0, at, :] * flags[b : b + 1]) - factor * summed

        block_loop(body)
        for step in range(1, layers):
            out_move(n, step).start()
        out_local(n).start()

    flags_a[0] = expand(pattern[...], 0, cols)
    expand_chunks(pattern[...], store_x(0))
    expand_chunks(keep[...], store_keep)
    flags_x[chunks] = jnp.ones_like(flags_x[chunks])
    for copy in panel_local:
        copy.wait()
    prepare_panel(0, col)
    for copy in piece_local:
        copy.wait()

    hand_on(0)
    send_x(1)
    for copy in flag_moves:
        copy.wait_recv()
    flags_a[1] = expand(flags_in[3], 0, cols)
    for slot in (1, 2, 3):
        expand_chunks(flags_in[slot - 1], store_x(slot))
    for copy in panel_moves:
        copy.wait_recv()
    prepare_panel(1, 1 - col)

    def advance(task, carry):
        @pl.when(task < tasks)
        def _():
            hand_on(task)

        @pl.when(task + 1 < chunks)
        def _():
            send_x(task + 1)

        @pl.when((task + 1 >= chunks) & (task + 1 < tasks))
        def _():
            send_f(task + 1)

        @pl.when(task - 1 < chunks)
        def _():
            finish_square(task - 1)

        @pl.when(task - 1 >= chunks)
        def _():
            finish_update(task - 1)

        return carry

    lax.fori_loop(1, tasks + 1, advance, 0)

    for copy in flag_moves + panel_moves:
        copy.wait_send()

    def drain(task, carry):
        for arrival in range(6):
            move(task, arrival, part(task, 0, 0)).wait_send()
        return carry

    lax.fori_loop(0, tasks, drain, 0)

    def drain_out(n, carry):
        for step in range(1, layers):
            out_move(n, step).wait()
        out_local(n).wait()
        return carry

    lax.fori_loop(0, chunks, drain_out, 0)


def fused(matrix, pattern, keep):
    rows, cols = matrix.shape
    layers = lax.axis_size("layer")
    block_rows, block_cols = pattern.shape
    block = rows // block_rows
    chunks = cols // layers // LANES
    tasks = 2 * chunks
    half = rows // 2
    wide = -(-block_cols // LANES) * LANES
    factor = 0.5 * DAMPING / (rows * lax.axis_size("row"))

    def padded(flags):
        return jnp.pad(flags.astype(jnp.float32), ((0, 0), (0, wide - block_cols)))

    vmem = pl.BlockSpec(memory_space=pltpu.VMEM)
    anywhere = pl.BlockSpec(memory_space=pl.ANY)
    dma = pltpu.SemaphoreType.DMA
    return pl.pallas_call(
        functools.partial(kernel, layers, block, factor),
        out_shape=jax.ShapeDtypeStruct((rows // layers, cols), jnp.float32),
        in_specs=[anywhere, vmem, vmem],
        out_specs=anywhere,
        scratch_shapes=[
            pltpu.VMEM((tasks, 4, rows, LANES), jnp.float32),
            pltpu.VMEM((2, rows, cols), jnp.float32),
            pltpu.VMEM((8, rows, half), jnp.bfloat16),
            pltpu.VMEM((8, rows, half), jnp.bfloat16),
            pltpu.VMEM((half, 2 * LANES), jnp.bfloat16),
            pltpu.VMEM((rows, 2 * LANES), jnp.float32),
            pltpu.VMEM((chunks, rows, LANES), jnp.float32),
            pltpu.VMEM((4, block_rows, wide), jnp.float32),
            pltpu.VMEM((2, block_rows, cols), jnp.float32),
            pltpu.VMEM((chunks + 1, 4, block_rows, LANES), jnp.float32),
            pltpu.VMEM((chunks, block_rows, LANES), jnp.float32),
            dma((tasks, 6)),
            dma((tasks, 6)),
            dma((4,)),
            dma((4,)),
            dma((4,)),
            dma((4,)),
            dma((chunks, max(layers - 1, 1))),
            dma((chunks, max(layers - 1, 1))),
            dma((4 + 2 * chunks,)),
        ],
        compiler_params=pltpu.CompilerParams(
            collective_id=0, has_side_effects=True, vmem_limit_bytes=67_000_000
        ),
    )(matrix, padded(pattern), padded(keep))


def local(matrix, pattern, keep):
    rows, cols = matrix.shape
    layers = lax.axis_size("layer")
    block = rows // pattern.shape[0]
    fits = (
        lax.axis_size("row") == 4
        and lax.axis_size("col") == 2
        and cols % (layers * LANES) == 0
        and cols // (layers * LANES) >= 3
        and LANES % block == 0
        and block % 16 == 0
        and rows % (16 * block) == 0
        and rows % (8 * layers) == 0
        and (rows // 2) % LANES == 0
        and rows * cols <= 1 << 21
    )
    return (fused if fits else plain)(matrix, pattern, keep)


def solution(mesh):
    placed = (P("row", "col"), P("row", "col"), P("row", "col"))
    return jax.shard_map(
        local, mesh=mesh, in_specs=placed, out_specs=P(("row", "layer"), "col"), check_vma=False
    )
```

time: 560 us -> 169 us (0.30)
  waiting for transfers between devices: 429 us -> 0 us
  Pallas kernels: 0 us -> 162 us
  local copies, waits for them, and re-layouts: 63.8 us -> 4.35 us
  matrix products: 34.9 us -> 0 us
  other arithmetic: 15.4 us -> 1.44 us
  between operations: 13.2 us -> 0.01 us
    reduce_scatter x2 -> x0, waiting for transfers between devices: 240 us -> none  [the longest x1 133 us: local(): lax.psum_scatter(by_layer.reshape(rows, cols), 'layer', scatter_dimension...]
    all_gather x3 -> x0, waiting for transfers between devices: 190 us -> none  [the longest x1 90.3 us: local(): lax.all_gather(layer_rows(sparse, layers, level), 'row', axis=0, tiled=True)]
    pallas_call x0 -> x1, Pallas kernels: none -> 162 us  [fused(): pl.pallas_call(functools.partial(kernel, layers, block, factor), out_shap...]
    mul x8 -> x0, local copies, waits for them, and re-layouts: 49.8 us -> none  [the longest x6 38.8 us: local(): matrix.reshape(block_rows, BS, block_cols, BS)]
    dot_general x2 -> x0, matrix products: 34.9 us -> none  [the longest x1 18.1 us: local(): jnp.dot(left_full, filtered_full, preferred_element_type=jnp.float32, pre...]
    mul x3 -> x0, other arithmetic: 9.69 us -> none  [the longest x2 6.53 us: local(): matrix.reshape(block_rows, BS, block_cols, BS)]
    unnamed x3 -> x1, local copies, waits for them, and re-layouts: 9.92 us -> 3.14 us
  transfers between devices with their start and end apart: 5 -> 0, of which waited for: 5 -> 0; matrix products, arithmetic and copies ran while one was open for 9% -> 0% of each run, Pallas kernels for 0% -> 0%
where the time goes in v1:
time: 169 us; the launch traced here: 168 us
  Pallas kernels  162 us (96%)
  local copies, waits for them, and re-layouts  4.35 us (3%)
    pallas_call x1, Pallas kernels, fused(): pl.pallas_call(functools.partial(kernel, layers, block, factor), out_shap...  162 us

profile of v1, /device:TPU:12, one launch (start us, length us, event | category | flops | bytes accessed | tf_op | source)
XLA Modules:
  0.0 167.9 jit_solution(16998698956281286736)
XLA Ops:
  0.0 0.7 convert_element_type.9
  0.7 0.6 pad.7.pattern
  1.3 0.7 convert_element_type.10
  2.1 0.6 pad.8.keep
  2.7 162.1 %shard_map.37 = f32[256,2048]{1,0:T(8,128)} custom-call(f32[1024,2048]{1,0:T(8,128)} %matrix.1, f32[32,128]{1,0:T(8,128)} %pad.7.pattern, f32[32,128]{1,0:T(8,128)} %pad.8.keep), custom_call_target="tpu_custom_call" | custom-call | tf_op jit(solution)/shard_map/pallas_call | solution.py:377
  164.8 3.1 %copy.5 = f32[256,2048]{1,0:T(8,128)} copy(f32[256,2048]{1,0:T(8,128)} %shard_map.37) | data formatting | bytes 4194304

commit v2 on v1

--- a/solution.py
+++ b/solution.py
@@ -109,7 +109,9 @@
         move(task, 2, part(task, 2, 1)).wait_recv()
         move(task, 5, part(task, 2, 1)).start()
 
-    send_x(0)
+    @pl.when(col == 0)
+    def _():
+        send_x(0)
 
     flag_moves = [
         remote(pattern, flags_in.at[n], flag_send.at[n], flag_recv.at[n], peer)
@@ -124,25 +126,27 @@
         return pl.ds(n * tall, tall)
 
     panel_moves = [
-        remote(matrix.at[band(n)], panel.at[1, band(n)], panel_send.at[n], panel_recv.at[n], twin)
+        remote(matrix.at[band(n)], panel.at[band(n)], panel_send.at[n], panel_recv.at[n], twin)
         for n in range(bands)
     ]
+    def own_panel(n):
+        return raw.at[chunks + n // 4, n % 4]
+
     panel_local = [
-        pltpu.make_async_copy(matrix.at[band(n)], panel.at[0, band(n)], local_sem.at[n])
-        for n in range(bands)
+        pltpu.make_async_copy(
+            matrix.at[:, pl.ds(n * LANES, LANES)], own_panel(n), local_sem.at[2 * chunks + n]
+        )
+        for n in range(cols // LANES)
     ]
     piece_local = [
         pltpu.make_async_copy(
             matrix.at[:, pl.ds(pl.multiple_of((level * chunks + n) * LANES, LANES), LANES)],
             raw.at[n, 0],
-            local_sem.at[bands + n],
+            local_sem.at[n],
         )
         for n in range(chunks)
     ]
-    for n in range(bands):
-        panel_local[n].start()
-        panel_moves[n].start()
-    for copy in piece_local:
+    for copy in panel_moves + panel_local + piece_local:
         copy.start()
 
     def expand(flags, first, width):
@@ -151,7 +155,7 @@
         start = (index - first) * block
         table = jnp.where((lane >= start) & (lane < start + block), 1.0, 0.0)
         return jnp.dot(
-            flags.astype(jnp.bfloat16), table.astype(jnp.bfloat16), preferred_element_type=jnp.float32
+            flags.astype(jnp.float32).astype(jnp.bfloat16), table.astype(jnp.bfloat16), preferred_element_type=jnp.float32
         )
 
     per_chunk = LANES // block
@@ -177,86 +181,40 @@
             place = slot * 2 + n % 2
 
             def body(i, carry):
-                flags = flags_a[side, pl.ds(pl.multiple_of(i * group, group), group), n * half : (n + 1) * half]
-                for b in range(group):
-                    at = pl.ds(pl.multiple_of((i * group + b) * block, block), block)
-                    values = panel[side, at, n * half : (n + 1) * half] * flags[b : b + 1]
-                    high, low = split(values)
-                    a_high[place, at] = high
-                    a_low[place, at] = low
+                base = pl.multiple_of(i * group, group)
+                for m in range(half // LANES):
+                    lanes = n * half + m * LANES
+                    flags = flags_a[side, pl.ds(base, group), lanes : lanes + LANES]
+                    for b in range(group):
+                        at = pl.ds(pl.multiple_of((i * group + b) * block, block), block)
+                        if side:
+                            values = panel[at, lanes : lanes + LANES]
+                        else:
+                            values = own_panel(lanes // LANES)[at, :]
+                        high, low = split(values * flags[b : b + 1])
+                        a_high[place, at, m * LANES : (m + 1) * LANES] = high
+                        a_low[place, at, m * LANES : (m + 1) * LANES] = low
                 return carry
 
             lax.fori_loop(0, block_rows // group, body, 0)
-
-    def take(task, slot, top):
-        which = task - (task // chunks) * (task - chunks)
-
-        def convert(i, carry):
-            first = top * (half // block) + i * group
-            flags = flags_x[which, slot, pl.ds(pl.multiple_of(first, group), group), :]
-            for b in range(group):
-                at = pl.ds(pl.multiple_of((first + b) * block, block), block)
-                to = pl.ds(pl.multiple_of((i * group + b) * block, block), block)
-                high, low = split(raw[task, slot, at, :] * flags[b : b + 1])
-                both[to, 0:LANES] = high
-                both[to, LANES : 2 * LANES] = low
-            return carry
-
-        lax.fori_loop(0, half // block // group, convert, 0)
-        place = slot * 2 + top
-
-        def multiply(i, carry):
-            at = pl.ds(pl.multiple_of(i * half, half), half)
-            total[at, :] += jnp.dot(
-                a_high[place, at, :], both[...], preferred_element_type=jnp.float32
-            ) + jnp.dot(a_low[place, at, :], both[...], preferred_element_type=jnp.float32)
-            return carry
-
-        lax.fori_loop(0, 2, multiply, 0)
-
-    def finish(task):
-        total[...] = jnp.zeros_like(total)
-
-        def present(g, carry):
-            take(task, g // 2 * (1 + g % 2), g % 2)
-            return carry
-
-        lax.fori_loop(0, 4, present, 0)
-        for arrival, slot, top in ((3, 2, 0), (1, 1, 1), (4, 3, 0), (5, 3, 1)):
-            move(task, arrival, part(task, slot, top)).wait_recv()
-            if arrival == 1:
-                late(task, 0)
-            if arrival == 5:
-                late(task, 2)
-
-    def late(task, base):
-        def body(g, carry):
-            take(task, (1 - base // 2) * (2 - g) + base // 2 * 3, g)
-            return carry
-
-        lax.fori_loop(0, 2, body, 0)
-
-    def block_loop(body):
-        def step(i, carry):
-            for b in range(group):
-                body(i, b)
-            return carry
-
-        lax.fori_loop(0, block_rows // group, step, 0)
 
     def at_block(i, b):
         return pl.ds(pl.multiple_of((i * group + b) * block, block), block)
 
-    def finish_square(task):
-        finish(task)
-
-        def body(i, b):
-            flags = flags_keep[task, pl.ds(pl.multiple_of(i * group, group), group), :]
-            at = at_block(i, b)
-            summed = total[at, 0:LANES] + total[at, LANES : 2 * LANES]
-            raw[task + chunks, 0, at, :] = summed * flags[b : b + 1]
-
-        block_loop(body)
+    def convert(task, slot, top):
+        which = task - (task // chunks) * (task - chunks)
+
+        def body(i, carry):
+            flags = flags_x[which, slot, pl.ds(pl.multiple_of(i * group, group), group), :]
+            for b in range(group):
+                at = at_block(i, b)
+                high, low = split(raw[task, slot, at, :] * flags[b : b + 1])
+                both[at, 0:LANES] = high
+                both[at, LANES : 2 * LANES] = low
+            return carry
+
+        steps = block_rows // group // 2
+        lax.fori_loop(top * steps, (top + 1) * steps, body, 0)
 
     def out_move(n, step):
         target = (level + step) % layers
@@ -274,36 +232,115 @@
         return pltpu.make_async_copy(
             staged.at[n, pl.ds(pl.multiple_of(level * share, share), share)],
             out.at[:, pl.ds(start, LANES)],
-            local_sem.at[bands + chunks + n],
-        )
-
-    def finish_update(task):
-        finish(task)
-        n = task - chunks
-
-        def body(i, b):
+            local_sem.at[chunks + n],
+        )
+
+    def finish_rows(task, tile):
+        steps = block_rows // group // 2
+
+        def square(i, carry):
+            flags = flags_keep[task, pl.ds(pl.multiple_of(i * group, group), group), :]
+            for b in range(group):
+                at = at_block(i, b)
+                summed = total[at, 0:LANES] + total[at, LANES : 2 * LANES]
+                raw[task + chunks, 0, at, :] = summed * flags[b : b + 1]
+            return carry
+
+        def update(i, carry):
+            n = task - chunks
             flags = flags_x[n, 0, pl.ds(pl.multiple_of(i * group, group), group), :]
-            at = at_block(i, b)
-            summed = total[at, 0:LANES] + total[at, LANES : 2 * LANES]
-            staged[n, at, :] = 1.5 * (raw[n, 0, at, :] * flags[b : b + 1]) - factor * summed
-
-        block_loop(body)
-        for step in range(1, layers):
-            out_move(n, step).start()
-        out_local(n).start()
+            for b in range(group):
+                at = at_block(i, b)
+                summed = total[at, 0:LANES] + total[at, LANES : 2 * LANES]
+                staged[n, at, :] = 1.5 * (raw[n, 0, at, :] * flags[b : b + 1]) - factor * summed
+            return carry
+
+        @pl.when(task < chunks)
+        def _():
+            lax.fori_loop(tile * steps, (tile + 1) * steps, square, 0)
+
+        @pl.when(task >= chunks)
+        def _():
+            lax.fori_loop(tile * steps, (tile + 1) * steps, update, 0)
+
+    def finish(task):
+        total[...] = jnp.zeros_like(total)
+
+        def pair(g, carry):
+            other = g % 2 * 2 + g // 2
+
+            @pl.when(g >= 2)
+            def _():
+                for slot, top, arrival in ((g, 0, g + 1), (other, 1, 4 * g - 7)):
+                    remote(
+                        part(task, slot, top), part(task, slot, top),
+                        send_sem.at[task, arrival], recv_sem.at[task, arrival], along_x,
+                    ).wait_recv()
+
+            convert(task, g, 0)
+            convert(task, other, 1)
+
+            def multiply(tile, carry):
+                at = pl.ds(pl.multiple_of(tile * half, half), half)
+                value = total[at, :]
+                for place, rows_of in ((g * 2, both.at[0:half]), (other * 2 + 1, both.at[half:rows])):
+                    for side in (a_high, a_low):
+                        value += jnp.dot(
+                            side[place, at, :], rows_of[...], preferred_element_type=jnp.float32
+                        )
+                total[at, :] = value
+
+                @pl.when(g == 3)
+                def _():
+                    finish_rows(task, tile)
+
+                return carry
+
+            lax.fori_loop(0, 2, multiply, 0)
+            return carry
+
+        lax.fori_loop(0, 4, pair, 0)
+
+        @pl.when(task >= chunks)
+        def _():
+            for step in range(1, layers):
+                out_move(task - chunks, step).start()
+            out_local(task - chunks).start()
+
+    def prepare_own():
+        for copy in panel_local:
+            copy.wait()
+        prepare_panel(0, col)
+
+    def send(task):
+        @pl.when(task < chunks)
+        def _():
+            send_x(task)
+
+        @pl.when((task >= chunks) & (task < tasks))
+        def _():
+            send_f(task)
 
     flags_a[0] = expand(pattern[...], 0, cols)
+
+    @pl.when(col == 1)
+    def _():
+        prepare_own()
+        send_x(0)
+
     expand_chunks(pattern[...], store_x(0))
     expand_chunks(keep[...], store_keep)
     flags_x[chunks] = jnp.ones_like(flags_x[chunks])
-    for copy in panel_local:
-        copy.wait()
-    prepare_panel(0, col)
     for copy in piece_local:
         copy.wait()
 
     hand_on(0)
     send_x(1)
+
+    @pl.when(col == 0)
+    def _():
+        prepare_own()
+
     for copy in flag_moves:
         copy.wait_recv()
     flags_a[1] = expand(flags_in[3], 0, cols)
@@ -312,31 +349,15 @@
     for copy in panel_moves:
         copy.wait_recv()
     prepare_panel(1, 1 - col)
+    finish(0)
 
     def advance(task, carry):
-        @pl.when(task < tasks)
-        def _():
-            hand_on(task)
-
-        @pl.when(task + 1 < chunks)
-        def _():
-            send_x(task + 1)
-
-        @pl.when((task + 1 >= chunks) & (task + 1 < tasks))
-        def _():
-            send_f(task + 1)
-
-        @pl.when(task - 1 < chunks)
-        def _():
-            finish_square(task - 1)
-
-        @pl.when(task - 1 >= chunks)
-        def _():
-            finish_update(task - 1)
-
+        hand_on(task)
+        send(task + 1)
+        finish(task)
         return carry
 
-    lax.fori_loop(1, tasks + 1, advance, 0)
+    lax.fori_loop(1, tasks, advance, 0)
 
     for copy in flag_moves + panel_moves:
         copy.wait_send()
@@ -365,11 +386,7 @@
     chunks = cols // layers // LANES
     tasks = 2 * chunks
     half = rows // 2
-    wide = -(-block_cols // LANES) * LANES
     factor = 0.5 * DAMPING / (rows * lax.axis_size("row"))
-
-    def padded(flags):
-        return jnp.pad(flags.astype(jnp.float32), ((0, 0), (0, wide - block_cols)))
 
     vmem = pl.BlockSpec(memory_space=pltpu.VMEM)
     anywhere = pl.BlockSpec(memory_space=pl.ANY)
@@ -378,16 +395,16 @@
         functools.partial(kernel, layers, block, factor),
         out_shape=jax.ShapeDtypeStruct((rows // layers, cols), jnp.float32),
         in_specs=[anywhere, vmem, vmem],
-        out_specs=anywhere,
+        out_specs=vmem,
         scratch_shapes=[
             pltpu.VMEM((tasks, 4, rows, LANES), jnp.float32),
-            pltpu.VMEM((2, rows, cols), jnp.float32),
+            pltpu.VMEM((rows, cols), jnp.float32),
             pltpu.VMEM((8, rows, half), jnp.bfloat16),
             pltpu.VMEM((8, rows, half), jnp.bfloat16),
-            pltpu.VMEM((half, 2 * LANES), jnp.bfloat16),
+            pltpu.VMEM((rows, 2 * LANES), jnp.bfloat16),
             pltpu.VMEM((rows, 2 * LANES), jnp.float32),
             pltpu.VMEM((chunks, rows, LANES), jnp.float32),
-            pltpu.VMEM((4, block_rows, wide), jnp.float32),
+            pltpu.VMEM((4, block_rows, block_cols), jnp.int32),
             pltpu.VMEM((2, block_rows, cols), jnp.float32),
             pltpu.VMEM((chunks + 1, 4, block_rows, LANES), jnp.float32),
             pltpu.VMEM((chunks, block_rows, LANES), jnp.float32),
@@ -399,12 +416,12 @@
             dma((4,)),
             dma((chunks, max(layers - 1, 1))),
             dma((chunks, max(layers - 1, 1))),
-            dma((4 + 2 * chunks,)),
+            dma((2 * chunks + cols // LANES,)),
         ],
         compiler_params=pltpu.CompilerParams(
-            collective_id=0, has_side_effects=True, vmem_limit_bytes=67_000_000
+            collective_id=0, has_side_effects=True, vmem_limit_bytes=52_000_000
         ),
-    )(matrix, padded(pattern), padded(keep))
+    )(matrix, pattern, keep)
 
 
 def local(matrix, pattern, keep):
@@ -422,6 +439,7 @@
         and rows % (8 * layers) == 0
         and (rows // 2) % LANES == 0
         and rows * cols <= 1 << 21
+        and layers <= 4
     )
     return (fused if fits else plain)(matrix, pattern, keep)
 

time: 169 us -> 156 us (0.923)
  Pallas kernels: 162 us -> 152 us
    pallas_call x1, Pallas kernels: 162 us -> 152 us  [fused(): pl.pallas_call(functools.partial(kernel, layers, block, factor), out_shap...]
where the time goes in v2:
time: 156 us; the launch traced here: 155 us
  Pallas kernels  152 us (97%)
  local copies, waits for them, and re-layouts  2.76 us (2%)
    pallas_call x1, Pallas kernels, fused(): pl.pallas_call(functools.partial(kernel, layers, block, factor), out_shap...  152 us

profile of v2, /device:TPU:12, one launch (start us, length us, event | category | flops | bytes accessed | tf_op | source)
XLA Modules:
  0.0 155.0 jit_solution(6007487501567356748)
XLA Ops:
  0.0 0.0 copy-start
  0.0 0.7 copy-done
  0.7 0.0 copy-start.1
  0.7 0.7 copy-done.1
  1.4 152.3 %shard_map.37 = f32[256,2048]{1,0:T(8,128)S(1)} custom-call(f32[1024,2048]{1,0:T(8,128)} %matrix.1, s32[32,64]{1,0:T(8,128)S(1)} %copy-done, s32[32,64]{1,0:T(8,128)S(1)} %copy-done.1), custom_call_target="tpu_custom_call" | custom-call | tf_op jit(solution)/shard_map/pallas_call | solution.py:394
  153.7 1.3 copy.5
Async XLA Ops:
  0.0 0.7 copy-start
  0.7 0.7 copy-start.1

commit v3 on v2

--- a/solution.py
+++ b/solution.py
@@ -49,9 +49,9 @@
 
 def kernel(
     layers, block, factor,
-    matrix, pattern, keep, out,
+    matrix, flags, out,
     raw, panel, a_high, a_low, both, total, staged, flags_in, flags_a, flags_x, flags_keep,
-    send_sem, recv_sem, panel_send, panel_recv, flag_send, flag_recv, out_send, out_recv, local_sem,
+    send_sem, recv_sem, panel_send, panel_recv, flag_send, flag_recv, flag_local_sem, out_send, out_recv, local_sem,
 ):
     rows, cols = matrix.shape
     chunks = cols // layers // LANES
@@ -109,17 +109,22 @@
         move(task, 2, part(task, 2, 1)).wait_recv()
         move(task, 5, part(task, 2, 1)).start()
 
-    @pl.when(col == 0)
+    @pl.when(col == 1)
     def _():
         send_x(0)
 
+    flag_local = [
+        pltpu.make_async_copy(flags.at[n], flags_in.at[4 + n], flag_local_sem.at[n]) for n in range(2)
+    ]
+    for copy in flag_local:
+        copy.start()
     flag_moves = [
-        remote(pattern, flags_in.at[n], flag_send.at[n], flag_recv.at[n], peer)
+        remote(flags.at[0], flags_in.at[n], flag_send.at[n], flag_recv.at[n], peer)
         for n, peer in enumerate((along_x, along_y, across, twin))
     ]
     for copy in flag_moves:
         copy.start()
-    bands = 4
+    bands = slices = 4
     tall = rows // bands
 
     def band(n):
@@ -236,7 +241,7 @@
         )
 
     def finish_rows(task, tile):
-        steps = block_rows // group // 2
+        steps = block_rows // group // slices
 
         def square(i, carry):
             flags = flags_keep[task, pl.ds(pl.multiple_of(i * group, group), group), :]
@@ -265,6 +270,7 @@
 
     def finish(task):
         total[...] = jnp.zeros_like(total)
+        first_tile = 1 - level * 2 // layers
 
         def pair(g, carry):
             other = g % 2 * 2 + g // 2
@@ -280,8 +286,9 @@
             convert(task, g, 0)
             convert(task, other, 1)
 
-            def multiply(tile, carry):
-                at = pl.ds(pl.multiple_of(tile * half, half), half)
+            def multiply(i, carry):
+                tile = (first_tile * (slices // 2) + i) % slices
+                at = pl.ds(pl.multiple_of(tile * tall, tall), tall)
                 value = total[at, :]
                 for place, rows_of in ((g * 2, both.at[0:half]), (other * 2 + 1, both.at[half:rows])):
                     for side in (a_high, a_low):
@@ -294,17 +301,22 @@
                 def _():
                     finish_rows(task, tile)
 
+                for step in range(1, layers):
+                    target = (level + step) % layers
+
+                    @pl.when((g == 3) & (task >= chunks) & (target * slices // layers == tile))
+                    def _():
+                        out_move(task - chunks, step).start()
+
                 return carry
 
-            lax.fori_loop(0, 2, multiply, 0)
+            lax.fori_loop(0, slices, multiply, 0)
             return carry
 
         lax.fori_loop(0, 4, pair, 0)
 
         @pl.when(task >= chunks)
         def _():
-            for step in range(1, layers):
-                out_move(task - chunks, step).start()
             out_local(task - chunks).start()
 
     def prepare_own():
@@ -321,25 +333,31 @@
         def _():
             send_f(task)
 
-    flags_a[0] = expand(pattern[...], 0, cols)
+    for copy in flag_local:
+        copy.wait()
+    flags_a[0] = expand(flags_in[4], 0, cols)
 
     @pl.when(col == 1)
     def _():
-        prepare_own()
+        hand_on(0)
+        send_x(1)
+
+    prepare_own()
+
+    @pl.when(col == 0)
+    def _():
         send_x(0)
 
-    expand_chunks(pattern[...], store_x(0))
-    expand_chunks(keep[...], store_keep)
+    expand_chunks(flags_in[4], store_x(0))
+    expand_chunks(flags_in[5], store_keep)
     flags_x[chunks] = jnp.ones_like(flags_x[chunks])
     for copy in piece_local:
         copy.wait()
 
-    hand_on(0)
-    send_x(1)
-
     @pl.when(col == 0)
     def _():
-        prepare_own()
+        hand_on(0)
+        send_x(1)
 
     for copy in flag_moves:
         copy.wait_recv()
@@ -394,7 +412,7 @@
     return pl.pallas_call(
         functools.partial(kernel, layers, block, factor),
         out_shape=jax.ShapeDtypeStruct((rows // layers, cols), jnp.float32),
-        in_specs=[anywhere, vmem, vmem],
+        in_specs=[anywhere, anywhere],
         out_specs=vmem,
         scratch_shapes=[
             pltpu.VMEM((tasks, 4, rows, LANES), jnp.float32),
@@ -404,7 +422,7 @@
             pltpu.VMEM((rows, 2 * LANES), jnp.bfloat16),
             pltpu.VMEM((rows, 2 * LANES), jnp.float32),
             pltpu.VMEM((chunks, rows, LANES), jnp.float32),
-            pltpu.VMEM((4, block_rows, block_cols), jnp.int32),
+            pltpu.VMEM((6, block_rows, block_cols), jnp.int32),
             pltpu.VMEM((2, block_rows, cols), jnp.float32),
             pltpu.VMEM((chunks + 1, 4, block_rows, LANES), jnp.float32),
             pltpu.VMEM((chunks, block_rows, LANES), jnp.float32),
@@ -414,6 +432,7 @@
             dma((4,)),
             dma((4,)),
             dma((4,)),
+            dma((2,)),
             dma((chunks, max(layers - 1, 1))),
             dma((chunks, max(layers - 1, 1))),
             dma((2 * chunks + cols // LANES,)),
@@ -421,7 +440,7 @@
         compiler_params=pltpu.CompilerParams(
             collective_id=0, has_side_effects=True, vmem_limit_bytes=52_000_000
         ),
-    )(matrix, pattern, keep)
+    )(matrix, jnp.stack([pattern, keep]))
 
 
 def local(matrix, pattern, keep):
@@ -439,7 +458,7 @@
         and rows % (8 * layers) == 0
         and (rows // 2) % LANES == 0
         and rows * cols <= 1 << 21
-        and layers <= 4
+        and layers in (1, 2, 4)
     )
     return (fused if fits else plain)(matrix, pattern, keep)
 

time: 156 us -> 154 us (0.987)
  Pallas kernels: 152 us -> 150 us
    pallas_call x1, Pallas kernels: 152 us -> 150 us  [fused(): pl.pallas_call(functools.partial(kernel, layers, block, factor), out_shap...]
where the time goes in v3:
time: 154 us; the launch traced here: 152 us
  Pallas kernels  150 us (97%)
    pallas_call x1, Pallas kernels, fused(): pl.pallas_call(functools.partial(kernel, layers, block, factor), out_shap...  150 us

profile of v3, /device:TPU:12, one launch (start us, length us, event | category | flops | bytes accessed | tf_op | source)
XLA Modules:
  0.0 152.4 jit_solution(3237113650465206510)
XLA Ops:
  0.0 0.7 pad_add_fusion.flags
  0.7 150.3 %shard_map.37 = f32[256,2048]{1,0:T(8,128)S(1)} custom-call(f32[1024,2048]{1,0:T(8,128)} %matrix.1, s32[2,32,64]{2,1,0:T(8,128)S(1)} %pad_add_fusion.flags), custom_call_target="tpu_custom_call" | custom-call | tf_op jit(solution)/shard_map/pallas_call | solution.py:412
  151.1 1.3 copy.5

commit v4 on v3

--- a/solution.py
+++ b/solution.py
@@ -50,14 +50,17 @@
 def kernel(
     layers, block, factor,
     matrix, flags, out,
-    raw, panel, a_high, a_low, both, total, staged, flags_in, flags_a, flags_x, flags_keep,
+    raw, panel, a_high, a_low, both, total, flags_in, flags_a, flags_x, flags_keep,
+    lent, lent_high, lent_low, flags_far, flags_lent_keep,
     send_sem, recv_sem, panel_send, panel_recv, flag_send, flag_recv, flag_local_sem, out_send, out_recv, local_sem,
+    lent_send, lent_recv, lent_local, twin_sem, far_sem,
 ):
     rows, cols = matrix.shape
     chunks = cols // layers // LANES
     tasks = 2 * chunks
     half = rows // 2
     share = rows // layers
+    extra = rows // 8
     block_rows = rows // block
     row = lax.axis_index("row")
     col = lax.axis_index("col")
@@ -85,29 +88,77 @@
         return raw.at[task, slot, pl.ds(top * half, half)]
 
     def move(task, arrival, source):
-        slot, top = ((1, 0), (1, 1), (2, 1), (2, 0), (3, 0), (3, 1))[arrival]
-        peer = along_x if arrival in (0, 1, 5) else along_y
+        slot, first, count = (
+            (1, extra, half - extra), (1, half, half), (2, half, half - extra), (2, 0, half),
+            (3, 0, half), (3, half, half), (1, 0, extra), (2, rows - extra, extra),
+        )[arrival]
+        peer = along_x if arrival in (0, 1, 5, 6) else along_y
         return remote(
-            source, part(task, slot, top), send_sem.at[task, arrival], recv_sem.at[task, arrival], peer
-        )
-
-    def own_x(task, top):
+            source(first, count), raw.at[task, slot, pl.ds(first, count)],
+            send_sem.at[task, arrival], recv_sem.at[task, arrival], peer,
+        )
+
+    def own_x(task):
         start = pl.multiple_of((level * chunks + task) * LANES, LANES)
-        return matrix.at[pl.ds(top * half, half), pl.ds(start, LANES)]
+        return lambda first, count: matrix.at[pl.ds(first, count), pl.ds(start, LANES)]
+
+    def in_slot(task, slot):
+        return lambda first, count: raw.at[task, slot, pl.ds(first, count)]
+
+    def send_first():
+        for task in range(chunks):
+            for arrival in (6, 7):
+                move(task, arrival, own_x(task)).start()
 
     def send_x(task):
-        for arrival, top in ((0, 0), (2, 1), (1, 1), (3, 0)):
-            move(task, arrival, own_x(task, top)).start()
+        for arrival in (0, 2, 1, 3):
+            move(task, arrival, own_x(task)).start()
 
     def send_f(task):
-        for arrival, top in ((0, 0), (2, 1), (1, 1), (3, 0)):
-            move(task, arrival, part(task, 0, top)).start()
+        for arrival in (0, 2, 1, 3):
+            move(task, arrival, in_slot(task, 0)).start()
 
     def hand_on(task):
-        move(task, 0, part(task, 1, 0)).wait_recv()
-        move(task, 4, part(task, 1, 0)).start()
-        move(task, 2, part(task, 2, 1)).wait_recv()
-        move(task, 5, part(task, 2, 1)).start()
+        move(task, 0, in_slot(task, 1)).wait_recv()
+        move(task, 4, in_slot(task, 1)).start()
+        move(task, 2, in_slot(task, 2)).wait_recv()
+        move(task, 5, in_slot(task, 2)).start()
+
+    def lent_rows(k):
+        return raw.at[pl.ds(0, chunks), 1 + k, pl.ds(k * (rows - extra), extra)]
+
+    def lent_slot(source, k):
+        return lent.at[pl.ds(source * chunks, chunks), pl.ds(k * extra, extra)]
+
+    def lend(k, step, source):
+        return remote(
+            lent_rows(k), lent_slot(source, k), lent_send.at[k, step - 1], lent_recv.at[k, step - 1],
+            {"layer": (level + step) % layers},
+        )
+
+    def lend_here(k):
+        return pltpu.make_async_copy(lent_rows(k), lent_slot(level, k), lent_local.at[k])
+
+    from_twin = panel.at[:, pl.ds(2 * extra, 2 * extra)]
+    lend_twin = remote(lent, from_twin, twin_sem.at[0], twin_sem.at[1], twin)
+
+    def lend_all():
+        for task in range(chunks):
+            for arrival in (6, 7):
+                move(task, arrival, in_slot(task, 1)).wait_recv()
+        for k in range(2):
+            for step in range(1, layers):
+                lend(k, step, level).start()
+            lend_here(k).start()
+
+    def pass_lent():
+        for k in range(2):
+            for step in range(1, layers):
+                lend(k, step, (level + layers - step) % layers).wait_recv()
+            lend_here(k).wait()
+        lend_twin.start()
+
+    send_first()
 
     @pl.when(col == 1)
     def _():
@@ -121,18 +172,21 @@
     flag_moves = [
         remote(flags.at[0], flags_in.at[n], flag_send.at[n], flag_recv.at[n], peer)
         for n, peer in enumerate((along_x, along_y, across, twin))
+    ] + [
+        remote(flags.at[1], flags_in.at[6 + n], flag_send.at[4 + n], flag_recv.at[4 + n], peer)
+        for n, peer in enumerate((along_x, along_y))
     ]
+    flags_on = remote(flags_in.at[pl.ds(0, 2)], flags_far, far_sem.at[0], far_sem.at[1], twin)
     for copy in flag_moves:
         copy.start()
-    bands = slices = 4
-    tall = rows // bands
-
-    def band(n):
-        return pl.ds(n * tall, tall)
+    slices = 4
+    tall = rows // slices
 
     panel_moves = [
-        remote(matrix.at[band(n)], panel.at[band(n)], panel_send.at[n], panel_recv.at[n], twin)
-        for n in range(bands)
+        remote(
+            matrix.at[:, pl.ds(n * LANES, LANES)], panel.at[n], panel_send.at[n], panel_recv.at[n], twin
+        )
+        for n in range(cols // LANES)
     ]
     def own_panel(n):
         return raw.at[chunks + n // 4, n % 4]
@@ -172,6 +226,11 @@
     def store_x(slot):
         def store(n, values):
             flags_x[n, slot] = values
+        return store
+
+    def store_lent(k):
+        def store(n, values):
+            flags_lent_keep[n, k] = values
         return store
 
     def store_keep(n, values):
@@ -193,7 +252,7 @@
                     for b in range(group):
                         at = pl.ds(pl.multiple_of((i * group + b) * block, block), block)
                         if side:
-                            values = panel[at, lanes : lanes + LANES]
+                            values = panel[lanes // LANES, at, :]
                         else:
                             values = own_panel(lanes // LANES)[at, :]
                         high, low = split(values * flags[b : b + 1])
@@ -221,11 +280,14 @@
         steps = block_rows // group // 2
         lax.fori_loop(top * steps, (top + 1) * steps, body, 0)
 
+    def staged(n):
+        return raw.at[n, 3]
+
     def out_move(n, step):
         target = (level + step) % layers
         start = pl.multiple_of((level * chunks + n) * LANES, LANES)
         return remote(
-            staged.at[n, pl.ds(pl.multiple_of(target * share, share), share)],
+            staged(n).at[pl.ds(pl.multiple_of(target * share, share), share)],
             out.at[:, pl.ds(start, LANES)],
             out_send.at[n, step - 1],
             out_recv.at[n, step - 1],
@@ -235,12 +297,12 @@
     def out_local(n):
         start = pl.multiple_of((level * chunks + n) * LANES, LANES)
         return pltpu.make_async_copy(
-            staged.at[n, pl.ds(pl.multiple_of(level * share, share), share)],
+            staged(n).at[pl.ds(pl.multiple_of(level * share, share), share)],
             out.at[:, pl.ds(start, LANES)],
             local_sem.at[chunks + n],
         )
 
-    def finish_rows(task, tile):
+    def finish_rows(task, second, tile):
         steps = block_rows // group // slices
 
         def square(i, carry):
@@ -257,18 +319,12 @@
             for b in range(group):
                 at = at_block(i, b)
                 summed = total[at, 0:LANES] + total[at, LANES : 2 * LANES]
-                staged[n, at, :] = 1.5 * (raw[n, 0, at, :] * flags[b : b + 1]) - factor * summed
+                raw[n, 3, at, :] = 1.5 * (raw[n, 0, at, :] * flags[b : b + 1]) - factor * summed
             return carry
 
-        @pl.when(task < chunks)
-        def _():
-            lax.fori_loop(tile * steps, (tile + 1) * steps, square, 0)
-
-        @pl.when(task >= chunks)
-        def _():
-            lax.fori_loop(tile * steps, (tile + 1) * steps, update, 0)
-
-    def finish(task):
+        lax.fori_loop(tile * steps, (tile + 1) * steps, update if second else square, 0)
+
+    def finish(task, second):
         total[...] = jnp.zeros_like(total)
         first_tile = 1 - level * 2 // layers
 
@@ -299,12 +355,12 @@
 
                 @pl.when(g == 3)
                 def _():
-                    finish_rows(task, tile)
-
-                for step in range(1, layers):
+                    finish_rows(task, second, tile)
+
+                for step in range(1, layers if second else 1):
                     target = (level + step) % layers
 
-                    @pl.when((g == 3) & (task >= chunks) & (target * slices // layers == tile))
+                    @pl.when((g == 3) & (target * slices // layers == tile))
                     def _():
                         out_move(task - chunks, step).start()
 
@@ -315,30 +371,61 @@
 
         lax.fori_loop(0, 4, pair, 0)
 
-        @pl.when(task >= chunks)
-        def _():
+        if second:
             out_local(task - chunks).start()
+
+    def prepare_lent():
+        for side, owner_col in ((0, col), (1, 1 - col)):
+            for n in range(cols // LANES):
+                owner = owner_col * (cols // rows) + n * LANES // rows
+                slot = (owner // 2 + y) % 2 * 2 + (owner % 2 + x) % 2
+                place = slot * 2 + n * LANES // half % 2
+                lanes = n * LANES % half
+                for k in range(2):
+                    for b in range(extra // block):
+                        flag = (side * 2 + k) * block_rows + k * (block_rows - extra // block) + b
+                        at = slice(k * extra + b * block, k * extra + (b + 1) * block)
+                        values = from_twin[n, at, :] if side else lent[n, at, :]
+                        values = values * panel[n, flag : flag + 1, :]
+                        high, low = split(values)
+                        lent_high[place, at, lanes : lanes + LANES] = high
+                        lent_low[place, at, lanes : lanes + LANES] = low
+
+    def square_lent(n):
+        total[0 : 2 * extra, :] = jnp.zeros((2 * extra, 2 * LANES), jnp.float32)
+
+        def pair(g, carry):
+            other = g % 2 * 2 + g // 2
+            convert(n, g, 0)
+            convert(n, other, 1)
+            value = total[0 : 2 * extra, :]
+            for place, rows_of in ((g * 2, both.at[0:half]), (other * 2 + 1, both.at[half:rows])):
+                for side in (lent_high, lent_low):
+                    value += jnp.dot(side[place], rows_of[...], preferred_element_type=jnp.float32)
+            total[0 : 2 * extra, :] = value
+            return carry
+
+        lax.fori_loop(0, 4, pair, 0)
+        for k in range(2):
+            for b in range(extra // block):
+                flag = k * (block_rows - extra // block) + b
+                at = slice(k * extra + b * block, k * extra + (b + 1) * block)
+                to = k * (rows - extra) + b * block
+                summed = total[at, 0:LANES] + total[at, LANES : 2 * LANES]
+                raw[n + chunks, 1 + k, to : to + block, :] = summed * flags_lent_keep[n, k, flag : flag + 1, :]
 
     def prepare_own():
         for copy in panel_local:
             copy.wait()
         prepare_panel(0, col)
 
-    def send(task):
-        @pl.when(task < chunks)
-        def _():
-            send_x(task)
-
-        @pl.when((task >= chunks) & (task < tasks))
-        def _():
-            send_f(task)
-
     for copy in flag_local:
         copy.wait()
     flags_a[0] = expand(flags_in[4], 0, cols)
 
     @pl.when(col == 1)
     def _():
+        lend_all()
         hand_on(0)
         send_x(1)
 
@@ -346,6 +433,7 @@
 
     @pl.when(col == 0)
     def _():
+        lend_all()
         send_x(0)
 
     expand_chunks(flags_in[4], store_x(0))
@@ -367,25 +455,69 @@
     for copy in panel_moves:
         copy.wait_recv()
     prepare_panel(1, 1 - col)
-    finish(0)
-
-    def advance(task, carry):
+    flags_on.start()
+    flags_on.wait_recv()
+    for k in range(2):
+        for side, source in ((0, flags_in), (1, flags_far)):
+            values = expand(source[k], 0, cols)
+            first_row = (side * 2 + k) * block_rows
+            for n in range(cols // LANES):
+                panel[n, first_row : first_row + block_rows, :] = values[:, n * LANES : (n + 1) * LANES]
+        expand_chunks(flags_in[6 + k], store_lent(k))
+    finish(0, False)
+
+    def first(task, carry):
         hand_on(task)
-        send(task + 1)
-        finish(task)
+
+        @pl.when(task + 1 < chunks)
+        def _():
+            send_x(task + 1)
+
+        @pl.when(task + 1 == chunks)
+        def _():
+            send_f(chunks)
+
+        @pl.when(task + 1 == chunks)
+        def _():
+            pass_lent()
+
+        finish(task, False)
         return carry
 
-    lax.fori_loop(1, tasks, advance, 0)
+    lax.fori_loop(1, chunks, first, 0)
+    lend_twin.wait_recv()
+    prepare_lent()
+    square_lent(0)
+
+    def second(task, carry):
+        hand_on(task)
+
+        @pl.when(task + 1 < tasks)
+        def _():
+            send_f(task + 1)
+            square_lent(task + 1 - chunks)
+
+        finish(task, True)
+        return carry
+
+    lax.fori_loop(chunks, tasks, second, 0)
+    flags_on.wait_send()
 
     for copy in flag_moves + panel_moves:
         copy.wait_send()
 
-    def drain(task, carry):
+    def drain(n, carry):
+        for arrival in range(8):
+            move(n, arrival, in_slot(n, 0)).wait_send()
         for arrival in range(6):
-            move(task, arrival, part(task, 0, 0)).wait_send()
+            move(n + chunks, arrival, in_slot(n, 0)).wait_send()
         return carry
 
-    lax.fori_loop(0, tasks, drain, 0)
+    lax.fori_loop(0, chunks, drain, 0)
+    for k in range(2):
+        for step in range(1, layers):
+            lend(k, step, level).wait_send()
+    lend_twin.wait_send()
 
     def drain_out(n, carry):
         for step in range(1, layers):
@@ -416,29 +548,38 @@
         out_specs=vmem,
         scratch_shapes=[
             pltpu.VMEM((tasks, 4, rows, LANES), jnp.float32),
-            pltpu.VMEM((rows, cols), jnp.float32),
+            pltpu.VMEM((cols // LANES, rows, LANES), jnp.float32),
             pltpu.VMEM((8, rows, half), jnp.bfloat16),
             pltpu.VMEM((8, rows, half), jnp.bfloat16),
             pltpu.VMEM((rows, 2 * LANES), jnp.bfloat16),
             pltpu.VMEM((rows, 2 * LANES), jnp.float32),
-            pltpu.VMEM((chunks, rows, LANES), jnp.float32),
-            pltpu.VMEM((6, block_rows, block_cols), jnp.int32),
+            pltpu.VMEM((8, block_rows, block_cols), jnp.int32),
             pltpu.VMEM((2, block_rows, cols), jnp.float32),
             pltpu.VMEM((chunks + 1, 4, block_rows, LANES), jnp.float32),
             pltpu.VMEM((chunks, block_rows, LANES), jnp.float32),
-            dma((tasks, 6)),
-            dma((tasks, 6)),
-            dma((4,)),
-            dma((4,)),
-            dma((4,)),
-            dma((4,)),
+            pltpu.VMEM((cols // LANES, rows // 4, LANES), jnp.float32),
+            pltpu.VMEM((8, rows // 4, half), jnp.bfloat16),
+            pltpu.VMEM((8, rows // 4, half), jnp.bfloat16),
+            pltpu.VMEM((2, block_rows, block_cols), jnp.int32),
+            pltpu.VMEM((chunks, 2, block_rows, LANES), jnp.float32),
+            dma((tasks, 8)),
+            dma((tasks, 8)),
+            dma((cols // LANES,)),
+            dma((cols // LANES,)),
+            dma((6,)),
+            dma((6,)),
             dma((2,)),
             dma((chunks, max(layers - 1, 1))),
             dma((chunks, max(layers - 1, 1))),
             dma((2 * chunks + cols // LANES,)),
+            dma((2, max(layers - 1, 1))),
+            dma((2, max(layers - 1, 1))),
+            dma((2,)),
+            dma((2,)),
+            dma((2,)),
         ],
         compiler_params=pltpu.CompilerParams(
-            collective_id=0, has_side_effects=True, vmem_limit_bytes=52_000_000
+            collective_id=0, has_side_effects=True, vmem_limit_bytes=54_200_000
         ),
     )(matrix, jnp.stack([pattern, keep]))
 
@@ -454,7 +595,7 @@
         and cols // (layers * LANES) >= 3
         and LANES % block == 0
         and block % 16 == 0
-        and rows % (16 * block) == 0
+        and rows % (32 * block) == 0
         and rows % (8 * layers) == 0
         and (rows // 2) % LANES == 0
         and rows * cols <= 1 << 21

time: 154 us -> 151 us (0.981)
  Pallas kernels: 150 us -> 148 us
    pallas_call x1, Pallas kernels: 150 us -> 148 us  [fused(): pl.pallas_call(functools.partial(kernel, layers, block, factor), out_shap...]
where the time goes in v4:
time: 151 us; the launch traced here: 150 us
  Pallas kernels  148 us (98%)
    pallas_call x1, Pallas kernels, fused(): pl.pallas_call(functools.partial(kernel, layers, block, factor), out_shap...  148 us

profile of v4, /device:TPU:12, one launch (start us, length us, event | category | flops | bytes accessed | tf_op | source)
XLA Modules:
  0.0 150.2 jit_solution(448271710086163735)
XLA Ops:
  0.0 0.7 pad_add_fusion.flags
  0.7 148.1 %shard_map.37 = f32[256,2048]{1,0:T(8,128)S(1)} custom-call(f32[1024,2048]{1,0:T(8,128)} %matrix.1, s32[2,32,64]{2,1,0:T(8,128)S(1)} %pad_add_fusion.flags), custom_call_target="tpu_custom_call" | custom-call | tf_op jit(solution)/shard_map/pallas_call | solution.py:544
  148.9 1.3 copy.5

commit v5 on v4

--- a/solution.py
+++ b/solution.py
@@ -242,7 +242,8 @@
         for n in range(cols // half):
             owner = owner_col * (cols // rows) + n // 2
             slot = (owner // 2 + y) % 2 * 2 + (owner % 2 + x) % 2
-            place = slot * 2 + n % 2
+            pair = slot if n % 2 == 0 else slot % 2 * 2 + slot // 2
+            left = n % 2 * half
 
             def body(i, carry):
                 base = pl.multiple_of(i * group, group)
@@ -256,8 +257,8 @@
                         else:
                             values = own_panel(lanes // LANES)[at, :]
                         high, low = split(values * flags[b : b + 1])
-                        a_high[place, at, m * LANES : (m + 1) * LANES] = high
-                        a_low[place, at, m * LANES : (m + 1) * LANES] = low
+                        a_high[pair, at, left + m * LANES : left + (m + 1) * LANES] = high
+                        a_low[pair, at, left + m * LANES : left + (m + 1) * LANES] = low
                 return carry
 
             lax.fori_loop(0, block_rows // group, body, 0)
@@ -342,31 +343,38 @@
             convert(task, g, 0)
             convert(task, other, 1)
 
+            def product(first, count):
+                at = pl.ds(pl.multiple_of(first, count), count)
+                value = total[at, :]
+                for side in (a_high, a_low):
+                    value += jnp.dot(side[g, at, :], both[...], preferred_element_type=jnp.float32)
+                total[at, :] = value
+
             def multiply(i, carry):
+                product(i * half, half)
+                return carry
+
+            def multiply_last(i, carry):
                 tile = (first_tile * (slices // 2) + i) % slices
-                at = pl.ds(pl.multiple_of(tile * tall, tall), tall)
-                value = total[at, :]
-                for place, rows_of in ((g * 2, both.at[0:half]), (other * 2 + 1, both.at[half:rows])):
-                    for side in (a_high, a_low):
-                        value += jnp.dot(
-                            side[place, at, :], rows_of[...], preferred_element_type=jnp.float32
-                        )
-                total[at, :] = value
-
-                @pl.when(g == 3)
-                def _():
-                    finish_rows(task, second, tile)
-
+                product(tile * tall, tall)
+                finish_rows(task, second, tile)
                 for step in range(1, layers if second else 1):
                     target = (level + step) % layers
 
-                    @pl.when((g == 3) & (target * slices // layers == tile))
+                    @pl.when(target * slices // layers == tile)
                     def _():
                         out_move(task - chunks, step).start()
 
                 return carry
 
-            lax.fori_loop(0, slices, multiply, 0)
+            @pl.when(g < 3)
+            def _():
+                lax.fori_loop(0, 2, multiply, 0)
+
+            @pl.when(g == 3)
+            def _():
+                lax.fori_loop(0, slices, multiply_last, 0)
+
             return carry
 
         lax.fori_loop(0, 4, pair, 0)
@@ -379,8 +387,8 @@
             for n in range(cols // LANES):
                 owner = owner_col * (cols // rows) + n * LANES // rows
                 slot = (owner // 2 + y) % 2 * 2 + (owner % 2 + x) % 2
-                place = slot * 2 + n * LANES // half % 2
-                lanes = n * LANES % half
+                pair = slot if n * LANES // half % 2 == 0 else slot % 2 * 2 + slot // 2
+                lanes = n * LANES % rows
                 for k in range(2):
                     for b in range(extra // block):
                         flag = (side * 2 + k) * block_rows + k * (block_rows - extra // block) + b
@@ -388,8 +396,8 @@
                         values = from_twin[n, at, :] if side else lent[n, at, :]
                         values = values * panel[n, flag : flag + 1, :]
                         high, low = split(values)
-                        lent_high[place, at, lanes : lanes + LANES] = high
-                        lent_low[place, at, lanes : lanes + LANES] = low
+                        lent_high[pair, at, lanes : lanes + LANES] = high
+                        lent_low[pair, at, lanes : lanes + LANES] = low
 
     def square_lent(n):
         total[0 : 2 * extra, :] = jnp.zeros((2 * extra, 2 * LANES), jnp.float32)
@@ -399,9 +407,8 @@
             convert(n, g, 0)
             convert(n, other, 1)
             value = total[0 : 2 * extra, :]
-            for place, rows_of in ((g * 2, both.at[0:half]), (other * 2 + 1, both.at[half:rows])):
-                for side in (lent_high, lent_low):
-                    value += jnp.dot(side[place], rows_of[...], preferred_element_type=jnp.float32)
+            for side in (lent_high, lent_low):
+                value += jnp.dot(side[g], both[...], preferred_element_type=jnp.float32)
             total[0 : 2 * extra, :] = value
             return carry
 
@@ -549,8 +556,8 @@
         scratch_shapes=[
             pltpu.VMEM((tasks, 4, rows, LANES), jnp.float32),
             pltpu.VMEM((cols // LANES, rows, LANES), jnp.float32),
-            pltpu.VMEM((8, rows, half), jnp.bfloat16),
-            pltpu.VMEM((8, rows, half), jnp.bfloat16),
+            pltpu.VMEM((4, rows, rows), jnp.bfloat16),
+            pltpu.VMEM((4, rows, rows), jnp.bfloat16),
             pltpu.VMEM((rows, 2 * LANES), jnp.bfloat16),
             pltpu.VMEM((rows, 2 * LANES), jnp.float32),
             pltpu.VMEM((8, block_rows, block_cols), jnp.int32),
@@ -558,8 +565,8 @@
             pltpu.VMEM((chunks + 1, 4, block_rows, LANES), jnp.float32),
             pltpu.VMEM((chunks, block_rows, LANES), jnp.float32),
             pltpu.VMEM((cols // LANES, rows // 4, LANES), jnp.float32),
-            pltpu.VMEM((8, rows // 4, half), jnp.bfloat16),
-            pltpu.VMEM((8, rows // 4, half), jnp.bfloat16),
+            pltpu.VMEM((4, rows // 4, rows), jnp.bfloat16),
+            pltpu.VMEM((4, rows // 4, rows), jnp.bfloat16),
             pltpu.VMEM((2, block_rows, block_cols), jnp.int32),
             pltpu.VMEM((chunks, 2, block_rows, LANES), jnp.float32),
             dma((tasks, 8)),

time: 151 us -> 151 us (level)
  no operation moved by 1% of the time
where the time goes in v5:
time: 151 us; the launch traced here: 150 us
  Pallas kernels  148 us (98%)
    pallas_call x1, Pallas kernels, fused(): pl.pallas_call(functools.partial(kernel, layers, block, factor), out_shap...  148 us

profile of v5, /device:TPU:12, one launch (start us, length us, event | category | flops | bytes accessed | tf_op | source)
XLA Modules:
  0.0 150.2 jit_solution(5864832003605127633)
XLA Ops:
  0.0 0.7 pad_add_fusion.flags
  0.7 148.1 %shard_map.37 = f32[256,2048]{1,0:T(8,128)S(1)} custom-call(f32[1024,2048]{1,0:T(8,128)} %matrix.1, s32[2,32,64]{2,1,0:T(8,128)S(1)} %pad_add_fusion.flags), custom_call_target="tpu_custom_call" | custom-call | tf_op jit(solution)/shard_map/pallas_call | solution.py:551
  148.9 1.3 copy.5
